TPU v7x, 8 devices: a whole 2x2x1 slice. The times are simulated.
8 devices in a mesh: dp: 1 (over z), tp: 2 (over y), ep: 4 (over x, core).
Axes of the slice: x: 2, y: 2, z: 1, core: 2. Of those that a mesh axis runs over, the one named last changes fastest.
Arguments:
- resid_in: bfloat16 [512, 7168], P(('dp', 'ep'))
- norm_scale: bfloat16 [7168], replicated
- w_router: bfloat16 [7168, 128], replicated
- w_gate: bfloat16 [128, 7168, 256], P('ep', None, 'tp')
- w_up: bfloat16 [128, 7168, 256], P('ep', None, 'tp')
- w_down: bfloat16 [128, 256, 7168], P('ep', 'tp')
- choice: int32 [512, 2], P(('dp', 'ep'))
Outputs:
- output: bfloat16 [512, 7168], P(('dp', 'ep'))
All inputs are finite; a program needn't handle non-finite values.
Results may differ from a plain program's by a relative error of at most 0.00572865.
Values are sent between devices in bfloat16 or wider.
A program may use at most 1 GiB of HBM per device.

v0:
```python
import functools

import jax
import jax.numpy as jnp
from jax import lax
from jax.experimental import pallas as pl
from jax.experimental.pallas import tpu as pltpu
from jax.sharding import PartitionSpec as P

NORM_EPS = 1e-5
MESH = pl.DeviceIdType.MESH
F32 = jnp.float32
BF16 = jnp.bfloat16
CAP = 4
GROUPS = 4
UP_STEPS = 7
UP_BUFS = 4
EARLY = 18
AHEAD = 3
LATE_BUFS = 6
UP_LAG = 2
DOWN_STEPS = 14
DOWN_BUFS = 4
DOWN_LAG = 2
TIERS = ((64, 160, 112), (64, 176, 112), (80, 176, 128), (96, 224, 128), (128, 256, 128))
DOWN_VMEM = (46 * 1024 * 1024, 46 * 1024 * 1024, 48 * 1024 * 1024, 52 * 1024 * 1024, 56 * 1024 * 1024)
VMEM_LIMIT = 60 * 1024 * 1024


def remote(src, dst, send_sem, recv_sem, device):
    return pltpu.make_async_remote_copy(src_ref=src, dst_ref=dst, send_sem=send_sem, recv_sem=recv_sem, device_id=device, device_id_type=MESH)


def place():
    dp, tp, ep = lax.axis_index('dp'), lax.axis_index('tp'), lax.axis_index('ep')
    return dp, tp, ep, ep // 2, ep % 2


def column(row):
    n = row.shape[1]
    eye = lax.broadcasted_iota(jnp.int32, (n, n), 0) == lax.broadcasted_iota(jnp.int32, (n, n), 1)
    return jnp.sum(jnp.where(eye, row.astype(F32), 0.0), axis=1, keepdims=True).astype(jnp.int32)


def up_kernel(x_ref, g_ref, wr_hbm, wg_hbm, wu_hbm, choice_ref, hid_ref, late_hbm, gate_ref, tab_ref, act_ref, flag_ref,
              u_ref, xs_ref, pick_ref, acc_ref, wbuf, logit_ref, ch_ref, wr_ref, stage_ref,
              w_sem, wr_sem, l_sem, c_s, c_r, own_s, own_r, x_s, x_r, y_s, y_r, dx_s, dx_r, dy_s, dy_r):
    dp, tp, ep, cx, core = place()
    tok, d_model = x_ref.shape
    half = d_model // 2
    steps = UP_STEPS
    cw = half // steps
    twin = (dp, tp, cx * 2 + (1 - core))
    across = (dp, tp, (1 - cx) * 2 + core)
    far_twin = (dp, tp, (1 - cx) * 2 + (1 - core))
    other_tp = (dp, 1 - tp, ep)
    far = (1 - cx) * 2 + core

    barrier = pltpu.get_barrier_semaphore()
    for peer in (twin, across, far_twin, other_tp):
        pl.semaphore_signal(barrier, inc=1, device_id=peer, device_id_type=MESH)

    def weight_copies(step, slot):
        out = []
        for h in range(2):
            rows = pl.ds(pl.multiple_of(h * half + step * cw, cw), cw)
            for m, w in enumerate((wg_hbm, wu_hbm)):
                out.append(pltpu.make_async_copy(w.at[0:EARLY, rows, :], wbuf.at[slot, :, h * cw:(h + 1) * cw, m * 128:(m + 1) * 128], w_sem.at[slot, h * 2 + m]))
        return out

    for b in range(2):
        for c in weight_copies(b, b):
            c.start()

    scale = g_ref[...].astype(F32).reshape(1, d_model)

    def norm_rows(r, carry):
        rows = pl.ds(pl.multiple_of(r * 16, 16), 16)
        xb = x_ref[rows, :].astype(F32)
        cen = xb - jnp.mean(xb, axis=-1, keepdims=True)
        var = jnp.mean(cen * cen, axis=-1, keepdims=True)
        u = (cen * lax.rsqrt(var + NORM_EPS) * scale).astype(BF16)
        for j in range(steps):
            for h in range(2):
                u_ref[j, h, ep, rows, :] = u[:, h * half + j * cw:h * half + (j + 1) * cw]
        return carry

    lax.fori_loop(0, tok // 16, norm_rows, 0)
    pl.semaphore_wait(barrier, 4)

    def choice_copy(n):
        peer = (across, far_twin, twin)[n]
        return remote(choice_ref, ch_ref.at[ep], c_s.at[n], c_r.at[n], peer)

    for n in range(3):
        choice_copy(n).start()

    own_copy = remote(u_ref.at[:, :, ep], u_ref.at[:, :, ep], own_s, own_r, twin)

    def x_copy(j):
        return remote(u_ref.at[j, tp, ep], u_ref.at[j, tp, ep], x_s.at[j], x_r.at[j], across)

    def y_copy(j):
        return remote(u_ref.at[j, tp, far], u_ref.at[j, tp, far], y_s.at[j], y_r.at[j], other_tp)

    def dx_copy(j):
        return remote(u_ref.at[j, tp, far], u_ref.at[j, tp, far], dx_s.at[j], dx_r.at[j], twin)

    def dy_copy(j):
        return remote(u_ref.at[j, 1 - tp, far], u_ref.at[j, 1 - tp, far], dy_s.at[j], dy_r.at[j], twin)

    def first_sends(j, carry):
        x_copy(j).start()
        return carry

    lax.fori_loop(0, AHEAD, first_sends, 0)
    own_copy.start()
    wr_copy = pltpu.make_async_copy(wr_hbm, wr_ref, wr_sem)
    wr_copy.start()
    for b in range(2, UP_BUFS):
        for c in weight_copies(b, b):
            c.start()
    ch_ref[ep] = choice_ref[...]
    acc_ref[...] = jnp.zeros_like(acc_ref)
    logit_ref[...] = jnp.zeros_like(logit_ref)
    for n in range(3):
        choice_copy(n).wait_recv()

    slots = pick_ref.shape[0]
    upper = jnp.where(lax.broadcasted_iota(jnp.int32, (tok, tok), 0) < lax.broadcasted_iota(jnp.int32, (tok, tok), 1), 1.0, 0.0).astype(BF16)
    ids = lax.broadcasted_iota(jnp.int32, (tok, tok), 0)
    lane16 = lax.broadcasted_iota(jnp.int32, (16, tok), 0)
    slot_iota = lax.broadcasted_iota(jnp.int32, (slots, tok), 0)
    most = jnp.zeros((16, 1), F32)
    load = jnp.zeros((tok, 1), F32)
    for g in range(GROUPS):
        c = [ch_ref[g, j:j + 1, :] for j in range(2)]
        hot = [jnp.where(ids == c[j], 1.0, 0.0) for j in range(2)]
        earlier = jnp.dot((hot[0] + hot[1]).astype(BF16), upper, preferred_element_type=F32)
        pos = [jnp.sum(earlier * hot[j], axis=0, keepdims=True).astype(jnp.int32) for j in range(2)]
        kept = [pos[j] < CAP for j in range(2)]
        keptf = [jnp.where(kept[j], 1.0, 0.0) for j in range(2)]
        owner = [c[j] // 32 for j in range(2)]
        mine = [jnp.where(lane16 == owner[j], keptf[j], 0.0) for j in range(2)]
        every = [jnp.where(lane16 == GROUPS, keptf[j], 0.0) for j in range(2)]
        some = jnp.maximum(keptf[0], keptf[1])
        tally = mine[0] + mine[1] + every[0] + every[1] + jnp.where(lane16 == GROUPS + 1, some, 0.0)
        before = jnp.dot(tally.astype(BF16), upper, preferred_element_type=F32)
        load = load + jnp.sum(hot[0] + hot[1], axis=1, keepdims=True)
        most = jnp.maximum(most, jnp.sum(tally, axis=1, keepdims=True))
        rank = [jnp.sum(before * mine[j], axis=0, keepdims=True) for j in range(2)]
        rank[1] = rank[1] + jnp.where(owner[0] == owner[1], keptf[0], 0.0)
        nrank = [before[GROUPS:GROUPS + 1, :], before[GROUPS:GROUPS + 1, :] + keptf[0]]
        for j in range(2):
            slot = jnp.where(kept[j] & (owner[j] == ep), (c[j] - ep * 32) * 16 + g * CAP + pos[j], -1)
            tab_ref[g, j:j + 1, :] = slot
            tab_ref[g, 2 + j:3 + j, :] = jnp.where(kept[j], owner[j] * 128 + rank[j].astype(jnp.int32), -1)
            tab_ref[g, 4 + j:5 + j, :] = jnp.where(kept[j], nrank[j].astype(jnp.int32), -1)
        tab_ref[g, 6:7, :] = jnp.where(some > 0.0, before[GROUPS + 1:GROUPS + 2, :].astype(jnp.int32), -1)
        tab_ref[g, 7:8, :] = jnp.zeros((1, tok), jnp.int32)
        pick_ref[:, g * tok:(g + 1) * tok] = jnp.where((slot_iota == tab_ref[g, 0:1, :]) | (slot_iota == tab_ref[g, 1:2, :]), 1.0, 0.0).astype(BF16)
    sub16 = lax.broadcasted_iota(jnp.int32, (16, 1), 0)
    fits = [jnp.where(sub16 < GROUPS, rows_c, jnp.where(sub16 == GROUPS, rows_n, jnp.where(sub16 == GROUPS + 1, rows_t, 0))).astype(F32) for rows_c, rows_n, rows_t in TIERS[:-1]]
    level = jnp.zeros((1, 1), F32)
    for f in fits:
        level = level + jnp.max(jnp.where(most > f, 1.0, 0.0), axis=0, keepdims=True)
    diag = ids == lax.broadcasted_iota(jnp.int32, (tok, tok), 1)
    act_ref[...] = jnp.sum(jnp.where(diag, load, 0.0), axis=0, keepdims=True).astype(jnp.int32)
    flag_ref[0] = jnp.max(level).astype(jnp.int32)

    wr_copy.wait()

    def late_copies(j):
        out = []
        for h in range(2):
            cols = pl.ds(pl.multiple_of(h * half + j * cw, cw), cw)
            out.append(pltpu.make_async_copy(stage_ref.at[j, h], late_hbm.at[:, cols], l_sem.at[j, h]))
        return out

    def main(i, carry):
        @pl.when(i < steps)
        def _():
            x_copy(i).wait_recv()
            y_copy(i).start()
            dx_copy(i).start()

        @pl.when(i + AHEAD < steps)
        def _():
            first_sends(i + AHEAD, 0)

        @pl.when((i >= UP_LAG) & (i < steps + UP_LAG))
        def _():
            j = i - UP_LAG
            y_copy(j).wait_recv()
            dy_copy(j).start()

        @pl.when(i >= UP_LAG + 1)
        def _():
            j = i - UP_LAG - 1
            slot = lax.rem(j, UP_BUFS)
            for h in range(2):
                kr = pl.ds(pl.multiple_of(h * half + j * cw, cw), cw)
                logit_ref[...] += jnp.dot(u_ref[j, h, ep], wr_ref[kr, :], preferred_element_type=F32)
            @pl.when(j == 0)
            def _():
                own_copy.wait_recv()
            dx_copy(j).wait_recv()
            dy_copy(j).wait_recv()
            for h in range(2):
                block = u_ref[j, h].reshape(GROUPS * tok, cw)
                rows_u = jnp.dot(pick_ref[...], block, preferred_element_type=F32).astype(BF16)
                xs_ref[:, h * cw:(h + 1) * cw] = rows_u[0:EARLY * 16]
                stage_ref[j, h] = rows_u[EARLY * 16:]
            for c in weight_copies(j, slot):
                c.wait()
            for c in late_copies(j):
                c.start()

            def experts(t, carry2):
                for z in range(3):
                    e = t * 3 + z
                    rows = pl.ds(pl.multiple_of(e * 16, 16), 16)
                    acc_ref[rows, :] += jnp.dot(xs_ref[rows, :], wbuf[slot, e], preferred_element_type=F32)
                return carry2

            lax.fori_loop(0, EARLY // 3, experts, 0)

            @pl.when(j + UP_BUFS < steps)
            def _():
                for c in weight_copies(j + UP_BUFS, slot):
                    c.start()
        return carry

    lax.fori_loop(0, steps + UP_LAG + 1, main, 0)

    gate_act = acc_ref[:, :128]
    hid_ref[...] = (gate_act * jax.nn.sigmoid(gate_act) * acc_ref[:, 128:]).astype(BF16)
    logits = logit_ref[...]
    ex = jnp.exp(logits - jnp.max(logits, axis=-1, keepdims=True))
    probs = ex / jnp.sum(ex, axis=-1, keepdims=True)
    lanes = lax.broadcasted_iota(jnp.int32, probs.shape, 1)
    picked = [jnp.sum(jnp.where(column(ch_ref[ep, j:j + 1, :]) == lanes, probs, 0.0), axis=-1, keepdims=True) for j in range(2)]
    for j in range(2):
        gate_ref[:, j:j + 1] = picked[j] / (picked[0] + picked[1])

    def last_waits(j, carry):
        for c in late_copies(j):
            c.wait()
        x_copy(j).wait_send()
        y_copy(j).wait_send()
        dx_copy(j).wait_send()
        dy_copy(j).wait_send()
        return carry

    lax.fori_loop(0, steps, last_waits, 0)
    own_copy.wait_send()
    for n in range(3):
        choice_copy(n).wait_send()


def late_kernel(act_ref, late_hbm, wg_hbm, wu_hbm, hid_ref, list_ref, late_ref, wbuf, w_sem, l_sem):
    ep = lax.axis_index('ep')
    local = wg_hbm.shape[0]
    hid_ref[...] = jnp.zeros_like(hid_ref)

    def scan(e, n):
        busy = act_ref[0, ep * local + e] > 0

        @pl.when(busy)
        def _():
            list_ref[n] = e
        return n + busy.astype(jnp.int32)

    count = lax.fori_loop(EARLY, local, scan, 0)

    def weight_copies(n):
        slot = lax.rem(n, LATE_BUFS)
        e = list_ref[n]
        return [pltpu.make_async_copy(w.at[e], wbuf.at[slot, :, m * 128:(m + 1) * 128], w_sem.at[slot, m]) for m, w in enumerate((wg_hbm, wu_hbm))]

    def start(n):
        @pl.when(n < count)
        def _():
            for c in weight_copies(n):
                c.start()

    rows_copy = pltpu.make_async_copy(late_hbm, late_ref, l_sem)
    rows_copy.start()
    for n in range(LATE_BUFS):
        start(n)
    rows_copy.wait()

    def step(n, carry):
        for c in weight_copies(n):
            c.wait()
        rows = pl.ds(pl.multiple_of((list_ref[n] - EARLY) * 16, 16), 16)
        both = jnp.dot(late_ref[rows, :], wbuf[lax.rem(n, LATE_BUFS)], preferred_element_type=F32)
        gate_act = both[:, :128]
        hid_ref[rows, :] = (gate_act * jax.nn.sigmoid(gate_act) * both[:, 128:]).astype(BF16)
        start(n + LATE_BUFS)
        return carry

    lax.fori_loop(0, count, step, 0)


def down_kernel(rows_c, rows_n, rows_t, early_ref, late_ref, x_ref, gate_ref, tab_ref, wd_hbm, out_ref,
                hid_ref, send_ref, land_ref, fwd_ref, yland_ref, done_ref, theirs_ref, qs_ref, w2buf, p_ref, s_ref, a_ref, b_ref, t_ref, e_ref,
                w_sem, q_s, q_r, f_s, f_r, o_s, o_r):
    dp, tp, ep, cx, core = place()
    local = wd_hbm.shape[0]
    tok, d_model = x_ref.shape
    half = d_model // 2
    steps = DOWN_STEPS
    cw = half // steps
    peers = [(1 - cx) * 2 + core, (1 - cx) * 2 + (1 - core), cx * 2 + (1 - core)]
    other_tp = (dp, 1 - tp, ep)

    barrier = pltpu.get_barrier_semaphore()
    for g in peers:
        pl.semaphore_signal(barrier, inc=1, device_id=(dp, tp, g), device_id_type=MESH)
    pl.semaphore_signal(barrier, inc=1, device_id=other_tp, device_id_type=MESH)

    def weight_copies(step, slot):
        out = []
        for h in range(2):
            cols = pl.ds(pl.multiple_of(h * half + step * cw, 128), cw)
            out.append(pltpu.make_async_copy(wd_hbm.at[:, :, cols], w2buf.at[slot, :, :, h * cw:(h + 1) * cw], w_sem.at[slot, h]))
        return out

    for c in weight_copies(0, 0):
        c.start()

    hid_ref[0:EARLY * 16, :] = early_ref[...]
    hid_ref[EARLY * 16:, :] = late_ref[...]
    all_rows = GROUPS * rows_c
    slots = qs_ref.shape[0]
    gap = 128 - rows_c
    slot_iota = lax.broadcasted_iota(jnp.int32, (slots, tok), 0)
    c_iota = lax.broadcasted_iota(jnp.int32, (rows_c, tok), 0)

    def key_of(r):
        for n in range(1, GROUPS):
            r = r + jnp.where(r >= n * rows_c + (n - 1) * gap, gap, 0)
        return r

    def onehot(rows, values):
        return jnp.where(rows == values, 1.0, 0.0).astype(BF16)

    def times_t(a, b):
        return lax.dot_general(a, b, (((1,), (1,)), ((), ())), preferred_element_type=F32)

    for g in range(GROUPS):
        total = jnp.zeros((rows_c, slots), F32)
        for j in range(2):
            total += times_t(onehot(c_iota + ep * 128, tab_ref[g, 2 + j:3 + j, :]), onehot(slot_iota, tab_ref[g, j:j + 1, :]))
        p_ref[g * rows_c:(g + 1) * rows_c, :] = total.astype(BF16)
    key_iota = key_of(lax.broadcasted_iota(jnp.int32, (all_rows, tok), 0))
    n_iota = lax.broadcasted_iota(jnp.int32, (rows_n, tok), 0)
    my_key = [tab_ref[ep, 2 + j:3 + j, :] for j in range(2)]
    my_n = [tab_ref[ep, 4 + j:5 + j, :] for j in range(2)]
    total = jnp.zeros((rows_n, all_rows), F32)
    for j in range(2):
        total += times_t(onehot(n_iota, my_n[j]), onehot(key_iota, my_key[j]))
    s_ref[...] = total.astype(BF16)

    def split_gates(keys, pos, dst):
        mat = jnp.where(pos[0] == keys, gate_ref[:, 0:1], 0.0) + jnp.where(pos[1] == keys, gate_ref[:, 1:2], 0.0)
        for z in range(3):
            part = mat.astype(BF16)
            dst[z] = part
            mat = mat - part.astype(F32)

    split_gates(key_of(lax.broadcasted_iota(jnp.int32, (tok, all_rows), 1)), [column(v) for v in my_key], a_ref)
    split_gates(lax.broadcasted_iota(jnp.int32, (tok, rows_n), 1), [column(v) for v in my_n], b_ref)
    my_t = tab_ref[ep, 6:7, :]
    t_ref[...] = onehot(lax.broadcasted_iota(jnp.int32, (rows_t, tok), 0), my_t)
    e_ref[...] = onehot(lax.broadcasted_iota(jnp.int32, (tok, rows_t), 1), column(my_t))
    some = column(my_t) >= 0
    for c in weight_copies(1, 1):
        c.start()
    pl.semaphore_wait(barrier, 4)

    def q_copy(k, n):
        return remote(send_ref.at[k, :, peers[n]], land_ref.at[k, :, ep], q_s.at[k, n], q_r.at[k, n], (dp, tp, peers[n]))

    def f_copy(k):
        return remote(fwd_ref.at[k], yland_ref.at[k], f_s.at[k], f_r.at[k], other_tp)

    def o_copy(k):
        return remote(done_ref.at[k], theirs_ref.at[k], o_s.at[k], o_r.at[k], other_tp)

    def main(i, carry):
        @pl.when(i < steps)
        def _():
            slot = lax.rem(i, DOWN_BUFS)
            for c in weight_copies(i, slot):
                c.wait()

            def experts(t, carry2):
                for z in range(4):
                    e = t * 4 + z
                    rows = pl.ds(pl.multiple_of(e * 16, 16), 16)
                    qs_ref[rows, :] = jnp.dot(hid_ref[rows, :], w2buf[slot, e], preferred_element_type=F32).astype(BF16)
                return carry2

            lax.fori_loop(0, local // 4, experts, 0)
            for h in range(2):
                send_ref[i, h] = jnp.dot(p_ref[...], qs_ref[:, h * cw:(h + 1) * cw], preferred_element_type=F32).astype(BF16).reshape(GROUPS, rows_c, cw)
            land_ref[i, :, ep] = send_ref[i, :, ep]

            for n in range(3):
                q_copy(i, n).start()

            @pl.when(i + DOWN_BUFS - 2 < steps)
            def _():
                for c in weight_copies(i + DOWN_BUFS - 2, lax.rem(i + DOWN_BUFS - 2, DOWN_BUFS)):
                    c.start()

        @pl.when((i >= DOWN_LAG) & (i < steps + DOWN_LAG))
        def _():
            k = i - DOWN_LAG
            for n in range(3):
                q_copy(k, n).wait_recv()
            block = land_ref[k, 1 - tp].reshape(GROUPS * rows_c, cw)
            fwd_ref[k] = jnp.dot(s_ref[...], block, preferred_element_type=F32).astype(BF16)
            f_copy(k).start()

        @pl.when((i >= 2 * DOWN_LAG) & (i < steps + 2 * DOWN_LAG))
        def _():
            k = i - 2 * DOWN_LAG
            mine = land_ref[k, tp].reshape(GROUPS * rows_c, cw)
            mix = jnp.dot(a_ref[2], mine, preferred_element_type=F32)
            mix += jnp.dot(a_ref[1], mine, preferred_element_type=F32)
            mix += jnp.dot(a_ref[0], mine, preferred_element_type=F32)
            f_copy(k).wait_recv()
            theirs = yland_ref[k]
            for z in (2, 1, 0):
                mix += jnp.dot(b_ref[z], theirs, preferred_element_type=F32)
            cols = pl.ds(pl.multiple_of(tp * half + k * cw, 128), cw)
            rows = (x_ref[:, cols].astype(F32) + mix).astype(BF16)
            done_ref[k] = jnp.dot(t_ref[...], rows, preferred_element_type=F32).astype(BF16)
            o_copy(k).start()
            out_ref[:, cols] = rows

        @pl.when(i >= 3 * DOWN_LAG)
        def _():
            k = i - 3 * DOWN_LAG
            cols = pl.ds(pl.multiple_of((1 - tp) * half + k * cw, 128), cw)
            o_copy(k).wait_recv()
            rows = jnp.dot(e_ref[...], theirs_ref[k], preferred_element_type=F32)
            out_ref[:, cols] = jnp.where(some, rows, x_ref[:, cols].astype(F32)).astype(BF16)
        return carry

    lax.fori_loop(0, steps + 3 * DOWN_LAG, main, 0)

    def last_waits(k, carry):
        for n in range(3):
            q_copy(k, n).wait_send()
        f_copy(k).wait_send()
        o_copy(k).wait_send()
        return carry

    lax.fori_loop(0, steps, last_waits, 0)


def run_up(x, g, wr, wg, wu, choice_t):
    tok, d_model = x.shape
    local = wg.shape[0]
    cw = d_model // 2 // UP_STEPS
    slots = local * GROUPS * CAP
    vm = pl.BlockSpec(memory_space=pltpu.VMEM)
    hbm = pl.BlockSpec(memory_space=pltpu.HBM)
    sem = pltpu.SemaphoreType.DMA
    return pl.pallas_call(
        up_kernel,
        out_shape=(
            jax.ShapeDtypeStruct((EARLY * 16, 128), BF16),
            jax.ShapeDtypeStruct((slots - EARLY * 16, d_model), BF16),
            jax.ShapeDtypeStruct((tok, 2), F32),
            jax.ShapeDtypeStruct((GROUPS, 8, tok), jnp.int32),
            jax.ShapeDtypeStruct((1, 128), jnp.int32),
            jax.ShapeDtypeStruct((1,), jnp.int32),
        ),
        in_specs=[vm, vm, hbm, hbm, hbm, vm],
        out_specs=(vm, hbm, vm, vm, vm, pl.BlockSpec(memory_space=pltpu.SMEM)),
        scratch_shapes=[
            pltpu.VMEM((UP_STEPS, 2, GROUPS, tok, cw), BF16),
            pltpu.VMEM((EARLY * 16, 2 * cw), BF16),
            pltpu.VMEM((slots, GROUPS * tok), BF16),
            pltpu.VMEM((EARLY * 16, 256), F32),
            pltpu.VMEM((UP_BUFS, EARLY, 2 * cw, 256), BF16),
            pltpu.VMEM((tok, 128), F32),
            pltpu.VMEM((GROUPS, 2, tok), jnp.int32),
            pltpu.VMEM(wr.shape, BF16),
            pltpu.VMEM((UP_STEPS, 2, slots - EARLY * 16, cw), BF16),
            sem((UP_BUFS, 4)), sem, sem((UP_STEPS, 2)), sem((3,)), sem((3,)), sem, sem,
        ] + [sem((UP_STEPS,))] * 8,
        compiler_params=pltpu.CompilerParams(collective_id=0, has_side_effects=True, vmem_limit_bytes=VMEM_LIMIT),
        name='up',
    )(x, g, wr, wg, wu, choice_t)


def run_late(act, late, wg, wu):
    d_model = late.shape[1]
    vm = pl.BlockSpec(memory_space=pltpu.VMEM)
    hbm = pl.BlockSpec(memory_space=pltpu.HBM)
    return pl.pallas_call(
        late_kernel,
        out_shape=jax.ShapeDtypeStruct((late.shape[0], 128), BF16),
        in_specs=[pl.BlockSpec(memory_space=pltpu.SMEM), hbm, hbm, hbm],
        out_specs=vm,
        scratch_shapes=[
            pltpu.SMEM((64,), jnp.int32),
            pltpu.VMEM(late.shape, BF16),
            pltpu.VMEM((LATE_BUFS, d_model, 256), BF16),
            pltpu.SemaphoreType.DMA((LATE_BUFS, 2)),
            pltpu.SemaphoreType.DMA,
        ],
        compiler_params=pltpu.CompilerParams(vmem_limit_bytes=44 * 1024 * 1024),
        name='late',
    )(act, late, wg, wu)


def run_down(tier, early, late, x, gate, tab, wd):
    rows_c, rows_n, rows_t = TIERS[tier]
    tok, d_model = x.shape
    local = wd.shape[0]
    cw = d_model // 2 // DOWN_STEPS
    slots = local * GROUPS * CAP
    vm = pl.BlockSpec(memory_space=pltpu.VMEM)
    hbm = pl.BlockSpec(memory_space=pltpu.HBM)
    sem = pltpu.SemaphoreType.DMA
    return pl.pallas_call(
        functools.partial(down_kernel, rows_c, rows_n, rows_t),
        out_shape=jax.ShapeDtypeStruct(x.shape, BF16),
        in_specs=[vm] * 5 + [hbm],
        out_specs=vm,
        scratch_shapes=[
            pltpu.VMEM((slots, 128), BF16),
            pltpu.VMEM((DOWN_STEPS, 2, GROUPS, rows_c, cw), BF16),
            pltpu.VMEM((DOWN_STEPS, 2, GROUPS, rows_c, cw), BF16),
            pltpu.VMEM((DOWN_STEPS, rows_n, cw), BF16),
            pltpu.VMEM((DOWN_STEPS, rows_n, cw), BF16),
            pltpu.VMEM((DOWN_STEPS, rows_t, cw), BF16),
            pltpu.VMEM((DOWN_STEPS, rows_t, cw), BF16),
            pltpu.VMEM((slots, 2 * cw), BF16),
            pltpu.VMEM((DOWN_BUFS, local, 128, 2 * cw), BF16),
            pltpu.VMEM((GROUPS * rows_c, slots), BF16),
            pltpu.VMEM((rows_n, GROUPS * rows_c), BF16),
            pltpu.VMEM((3, tok, GROUPS * rows_c), BF16),
            pltpu.VMEM((3, tok, rows_n), BF16),
            pltpu.VMEM((rows_t, tok), BF16),
            pltpu.VMEM((tok, rows_t), BF16),
            sem((DOWN_BUFS, 2)), sem((DOWN_STEPS, 3)), sem((DOWN_STEPS, 3)),
            sem((DOWN_STEPS,)), sem((DOWN_STEPS,)), sem((DOWN_STEPS,)), sem((DOWN_STEPS,)),
        ],
        compiler_params=pltpu.CompilerParams(collective_id=1 + tier, has_side_effects=True, vmem_limit_bytes=DOWN_VMEM[tier]),
        name='down%d_%d' % (rows_c, rows_n),
    )(early, late, x, gate, tab, wd)


def solution(mesh):
    row_spec = P(('dp', 'ep'), None)

    def device_step(resid_in, norm_scale, w_router, w_gate, w_up, w_down, choice):
        early, rows_late, gate, tab, act, flag = run_up(resid_in, norm_scale, w_router, w_gate, w_up, choice.T)
        late = run_late(act, rows_late, w_gate, w_up)
        return lax.switch(flag[0], [functools.partial(run_down, t) for t in range(len(TIERS))], early, late, resid_in, gate, tab, w_down)

    return jax.shard_map(device_step, mesh=mesh, in_specs=(row_spec, P(None), P(None, None), P('ep', None, 'tp'), P('ep', None, 'tp'), P('ep', 'tp', None), row_spec), out_specs=row_spec, check_vma=False)
```

profile of v0, /device:TPU:0, one launch (start us, length us, event | category | flops | bytes accessed | tf_op | source)
XLA Modules:
  0.0 115.1 jit_solution(15935239192821015090)
XLA Ops:
  0.0 42.4 %up.1 = (bf16[288,128]{1,0:T(8,128)(2,1)S(1)}, bf16[224,7168]{1,0:T(8,128)(2,1)}, f32[128,2]{1,0:T(8,128)S(1)}, s32[4,8,128]{2,1,0:T(8,128)S(1)}, s32[1,128]{1,0:T(1,128)}, /*index=5*/s32[1]{0:T(128)}) custom-call(bf16[128,7168]{1,0:T(8,128)(2,1)} %x_ref.1, bf16[7168]{0:T(1024)(128)(2,1)} %g_ref.1, bf16[7168,128]{1,0:T(8,128)(2,1)} %wr_hbm.1, ...), custom_call_target="tpu_custom_call" | custom-call | tf_op jit(solution)/shard_map/up/pallas_call | solution.py:474
  43.0 0.0 copy-start
  43.0 1.9 %copy-done = bf16[224,7168]{1,0:T(8,128)(2,1)S(1)} copy-done((bf16[224,7168]{1,0:T(8,128)(2,1)S(1)}, bf16[224,7168]{1,0:T(8,128)(2,1)}, u32[]{:S(2)}) %copy-start) | copy-done | bytes 3211288
  44.9 0.0 copy-start.1
  44.9 0.6 copy-done.1
  45.5 0.0 copy-start.2
  45.5 11.4 %late.1 = bf16[224,128]{1,0:T(8,128)(2,1)S(1)} custom-call(s32[1,128]{1,0:T(1,128)S(1)} %copy-done.1, bf16[224,7168]{1,0:T(8,128)(2,1)S(1)} %copy-done, bf16[32,7168,128]{2,1,0:T(8,128)(2,1)} %wg_hbm.3, bf16[32,7168,128]{2,1,0:T(8,128)(2,1)} %wu_hbm.3), custom_call_target="tpu_custom_call" | custom-call | tf_op jit(solution)/shard_map/late/pallas_call | solution.py:507
  56.9 0.0 copy-done.2
  56.9 56.9 %conditional.1 = (bf16[128,7168]{1,0:T(8,128)(2,1)S(1)}) conditional(s32[]{:T(128)} %bitcast.1, (bf16[288,128]{1,0:T(8,128)(2,1)S(1)}, bf16[224,128]{1,0:T(8,128)(2,1)S(1)}, bf16[128,7168]{1,0:T(8,128)(2,1)S(1)}, f32[128,2]{1,0:T(8,128)S(1)}, s32[4,8,128]{2,1,0:T(8,128)S(1)}, ...), branch_computations={%region_0.0_spmd, %region_1.0_spmd, %region_2.0_spmd, %region_3.0_... | conditional | bytes 8 | solution.py:568
  57.0 56.9 %down64_160.1 = bf16[128,7168]{1,0:T(8,128)(2,1)S(1)} custom-call(bf16[288,128]{1,0:T(8,128)(2,1)S(1)} %get-tuple-element.62.early_ref, bf16[224,128]{1,0:T(8,128)(2,1)S(1)} %get-tuple-element.70.late_ref, bf16[128,7168]{1,0:T(8,128)(2,1)S(1)} %get-tuple-element.72.x_ref, f32[128,2]{1,0:T(8,128)S(1)} %get-tuple-element.74.gate_ref, ...), custom_call_target="tpu_custom_call" | custom-call | tf_op jit(solution)/shard_map/cond/branch_0_fun/down64_160/pallas_call | solution.py:533
  113.9 1.2 %copy.24 = bf16[128,7168]{1,0:T(8,128)(2,1)} copy(bf16[128,7168]{1,0:T(8,128)(2,1)S(1)} %get-tuple-element.113) | data formatting | bytes 3670016
Async XLA Ops:
  43.0 1.9 %copy-start = (bf16[224,7168]{1,0:T(8,128)(2,1)S(1)}, bf16[224,7168]{1,0:T(8,128)(2,1)}, u32[]{:S(2)}) copy-start(bf16[224,7168]{1,0:T(8,128)(2,1)} %get-tuple-element.110.late_hbm) | copy-start | bytes 9633796
  44.9 0.6 copy-start.1
  45.5 11.4 %copy-start.2 = (bf16[128,7168]{1,0:T(8,128)(2,1)S(1)}, bf16[128,7168]{1,0:T(8,128)(2,1)}, u32[]{:S(2)}) copy-start(bf16[128,7168]{1,0:T(8,128)(2,1)} %x_ref.1) | copy-start | bytes 5505028
where the time goes:
time: 117 us; the launch traced here: 115 us
  Pallas kernels  111 us (95%)
  local copies, waits for them, and re-layouts  3.75 us (3%)
    pallas_call x1, Pallas kernels, run_down(): pl.pallas_call(functools.partial(down_kernel, rows_c, rows_n, rows_t), ou...  56.9 us
    pallas_call x1, Pallas kernels, run_up(): pl.pallas_call(up_kernel, out_shape=(jax.ShapeDtypeStruct((EARLY * 16, 12...  42.4 us
    pallas_call x1, Pallas kernels, run_late(): pl.pallas_call(late_kernel, out_shape=jax.ShapeDtypeStruct((late.shape[0]...  11.4 us
    unnamed x7, local copies, waits for them, and re-layouts  3.75 us

commit v1 on v0

--- a/solution.py
+++ b/solution.py
@@ -15,7 +15,7 @@
 GROUPS = 4
 UP_STEPS = 7
 UP_BUFS = 4
-EARLY = 18
+EARLY = 20
 AHEAD = 3
 LATE_BUFS = 6
 UP_LAG = 2
@@ -217,13 +217,13 @@
                 c.start()
 
             def experts(t, carry2):
-                for z in range(3):
-                    e = t * 3 + z
+                for z in range(4):
+                    e = t * 4 + z
                     rows = pl.ds(pl.multiple_of(e * 16, 16), 16)
                     acc_ref[rows, :] += jnp.dot(xs_ref[rows, :], wbuf[slot, e], preferred_element_type=F32)
                 return carry2
 
-            lax.fori_loop(0, EARLY // 3, experts, 0)
+            lax.fori_loop(0, EARLY // 4, experts, 0)
 
             @pl.when(j + UP_BUFS < steps)
             def _():
@@ -390,6 +390,15 @@
         return remote(done_ref.at[k], theirs_ref.at[k], o_s.at[k], o_r.at[k], other_tp)
 
     def main(i, carry):
+        @pl.when((i >= DOWN_LAG) & (i < steps + DOWN_LAG))
+        def _():
+            k = i - DOWN_LAG
+            for n in range(3):
+                q_copy(k, n).wait_recv()
+            block = land_ref[k, 1 - tp].reshape(GROUPS * rows_c, cw)
+            fwd_ref[k] = jnp.dot(s_ref[...], block, preferred_element_type=F32).astype(BF16)
+            f_copy(k).start()
+
         @pl.when(i < steps)
         def _():
             slot = lax.rem(i, DOWN_BUFS)
@@ -415,15 +424,6 @@
             def _():
                 for c in weight_copies(i + DOWN_BUFS - 2, lax.rem(i + DOWN_BUFS - 2, DOWN_BUFS)):
                     c.start()
-
-        @pl.when((i >= DOWN_LAG) & (i < steps + DOWN_LAG))
-        def _():
-            k = i - DOWN_LAG
-            for n in range(3):
-                q_copy(k, n).wait_recv()
-            block = land_ref[k, 1 - tp].reshape(GROUPS * rows_c, cw)
-            fwd_ref[k] = jnp.dot(s_ref[...], block, preferred_element_type=F32).astype(BF16)
-            f_copy(k).start()
 
         @pl.when((i >= 2 * DOWN_LAG) & (i < steps + 2 * DOWN_LAG))
         def _():
@@ -516,7 +516,7 @@
             pltpu.SemaphoreType.DMA((LATE_BUFS, 2)),
             pltpu.SemaphoreType.DMA,
         ],
-        compiler_params=pltpu.CompilerParams(vmem_limit_bytes=44 * 1024 * 1024),
+        compiler_params=pltpu.CompilerParams(vmem_limit_bytes=60 * 1024 * 1024),
         name='late',
     )(act, late, wg, wu)
 

time: 117 us -> 119 us (1.017); the launches traced: 115 us -> 118 us
  Pallas kernels: 111 us -> 117 us
  local copies, waits for them, and re-layouts: 3.75 us -> 1.24 us
    pallas_call x1, Pallas kernels: 56.9 us -> 62.8 us  [run_down(): pl.pallas_call(functools.partial(down_kernel, rows_c, rows_n, rows_t), ou...]
    unnamed x7 -> x3, local copies, waits for them, and re-layouts: 3.75 us -> 1.24 us
where the time goes in v1:
time: 119 us; the launch traced here: 118 us
  Pallas kernels  117 us (98%)
  local copies, waits for them, and re-layouts  1.24 us (1%)
    pallas_call x1, Pallas kernels, run_down(): pl.pallas_call(functools.partial(down_kernel, rows_c, rows_n, rows_t), ou...  62.8 us
    pallas_call x1, Pallas kernels, run_up(): pl.pallas_call(up_kernel, out_shape=(jax.ShapeDtypeStruct((EARLY * 16, 12...  42.5 us
    pallas_call x1, Pallas kernels, run_late(): pl.pallas_call(late_kernel, out_shape=jax.ShapeDtypeStruct((late.shape[0]...  11.2 us

profile of v1, /device:TPU:0, one launch (start us, length us, event | category | flops | bytes accessed | tf_op | source)
XLA Modules:
  0.0 118.4 jit_solution(9901376041410566048)
XLA Ops:
  0.0 42.5 %up.1 = (bf16[320,128]{1,0:T(8,128)(2,1)S(1)}, bf16[192,7168]{1,0:T(8,128)(2,1)}, f32[128,2]{1,0:T(8,128)S(1)}, s32[4,8,128]{2,1,0:T(8,128)S(1)}, s32[1,128]{1,0:T(1,128)}, /*index=5*/s32[1]{0:T(128)}) custom-call(bf16[128,7168]{1,0:T(8,128)(2,1)} %x_ref.1, bf16[7168]{0:T(1024)(128)(2,1)} %g_ref.1, bf16[7168,128]{1,0:T(8,128)(2,1)} %wr_hbm.1, ...), custom_call_target="tpu_custom_call" | custom-call | tf_op jit(solution)/shard_map/up/pallas_call | solution.py:474
  43.1 0.0 copy-start
  43.1 11.2 %late.1 = bf16[192,128]{1,0:T(8,128)(2,1)S(1)} custom-call(s32[1,128]{1,0:T(1,128)} %get-tuple-element.109.act_ref, bf16[192,7168]{1,0:T(8,128)(2,1)} %get-tuple-element.110.late_hbm, bf16[32,7168,128]{2,1,0:T(8,128)(2,1)} %wg_hbm.3, bf16[32,7168,128]{2,1,0:T(8,128)(2,1)} %wu_hbm.3), custom_call_target="tpu_custom_call" | custom-call | tf_op jit(solution)/shard_map/late/pallas_call | solution.py:507
  54.3 0.0 copy-done
  54.3 62.9 %conditional.1 = (bf16[128,7168]{1,0:T(8,128)(2,1)S(1)}) conditional(s32[]{:T(128)} %bitcast.1, (bf16[320,128]{1,0:T(8,128)(2,1)S(1)}, bf16[192,128]{1,0:T(8,128)(2,1)S(1)}, bf16[128,7168]{1,0:T(8,128)(2,1)S(1)}, f32[128,2]{1,0:T(8,128)S(1)}, s32[4,8,128]{2,1,0:T(8,128)S(1)}, ...), branch_computations={%region_0.0_spmd, %region_1.0_spmd, %region_2.0_spmd, %region_3.0_... | conditional | bytes 8 | solution.py:568
  54.3 62.8 %down64_176.1 = bf16[128,7168]{1,0:T(8,128)(2,1)S(1)} custom-call(bf16[320,128]{1,0:T(8,128)(2,1)S(1)} %get-tuple-element.77.early_ref, bf16[192,128]{1,0:T(8,128)(2,1)S(1)} %get-tuple-element.78.late_ref, bf16[128,7168]{1,0:T(8,128)(2,1)S(1)} %get-tuple-element.79.x_ref, f32[128,2]{1,0:T(8,128)S(1)} %get-tuple-element.80.gate_ref, ...), custom_call_target="tpu_custom_call" | custom-call | tf_op jit(solution)/shard_map/cond/branch_1_fun/down64_176/pallas_call | solution.py:533
  117.2 1.2 %copy.24 = bf16[128,7168]{1,0:T(8,128)(2,1)} copy(bf16[128,7168]{1,0:T(8,128)(2,1)S(1)} %get-tuple-element.113) | data formatting | bytes 3670016
Async XLA Ops:
  43.1 11.2 %copy-start = (bf16[128,7168]{1,0:T(8,128)(2,1)S(1)}, bf16[128,7168]{1,0:T(8,128)(2,1)}, u32[]{:S(2)}) copy-start(bf16[128,7168]{1,0:T(8,128)(2,1)} %x_ref.1) | copy-start | bytes 5505028

commit v2 on v0

--- a/solution.py
+++ b/solution.py
@@ -15,7 +15,7 @@
 GROUPS = 4
 UP_STEPS = 7
 UP_BUFS = 4
-EARLY = 18
+EARLY = 20
 AHEAD = 3
 LATE_BUFS = 6
 UP_LAG = 2
@@ -217,13 +217,13 @@
                 c.start()
 
             def experts(t, carry2):
-                for z in range(3):
-                    e = t * 3 + z
+                for z in range(4):
+                    e = t * 4 + z
                     rows = pl.ds(pl.multiple_of(e * 16, 16), 16)
                     acc_ref[rows, :] += jnp.dot(xs_ref[rows, :], wbuf[slot, e], preferred_element_type=F32)
                 return carry2
 
-            lax.fori_loop(0, EARLY // 3, experts, 0)
+            lax.fori_loop(0, EARLY // 4, experts, 0)
 
             @pl.when(j + UP_BUFS < steps)
             def _():
@@ -516,7 +516,7 @@
             pltpu.SemaphoreType.DMA((LATE_BUFS, 2)),
             pltpu.SemaphoreType.DMA,
         ],
-        compiler_params=pltpu.CompilerParams(vmem_limit_bytes=44 * 1024 * 1024),
+        compiler_params=pltpu.CompilerParams(vmem_limit_bytes=60 * 1024 * 1024),
         name='late',
     )(act, late, wg, wu)
 

time: 117 us -> 113 us (0.966); the launches traced: 115 us -> 112 us
  local copies, waits for them, and re-layouts: 3.75 us -> 1.24 us
    unnamed x7 -> x3, local copies, waits for them, and re-layouts: 3.75 us -> 1.24 us
where the time goes in v2:
time: 113 us; the launch traced here: 112 us
  Pallas kernels  111 us (98%)
  local copies, waits for them, and re-layouts  1.24 us (1%)
    pallas_call x1, Pallas kernels, run_down(): pl.pallas_call(functools.partial(down_kernel, rows_c, rows_n, rows_t), ou...  55.9 us
    pallas_call x1, Pallas kernels, run_up(): pl.pallas_call(up_kernel, out_shape=(jax.ShapeDtypeStruct((EARLY * 16, 12...  42.5 us
    pallas_call x1, Pallas kernels, run_late(): pl.pallas_call(late_kernel, out_shape=jax.ShapeDtypeStruct((late.shape[0]...  12.1 us

profile of v2, /device:TPU:0, one launch (start us, length us, event | category | flops | bytes accessed | tf_op | source)
XLA Modules:
  0.0 112.4 jit_solution(15878485550060578526)
XLA Ops:
  0.0 42.5 %up.1 = (bf16[320,128]{1,0:T(8,128)(2,1)S(1)}, bf16[192,7168]{1,0:T(8,128)(2,1)}, f32[128,2]{1,0:T(8,128)S(1)}, s32[4,8,128]{2,1,0:T(8,128)S(1)}, s32[1,128]{1,0:T(1,128)}, /*index=5*/s32[1]{0:T(128)}) custom-call(bf16[128,7168]{1,0:T(8,128)(2,1)} %x_ref.1, bf16[7168]{0:T(1024)(128)(2,1)} %g_ref.1, bf16[7168,128]{1,0:T(8,128)(2,1)} %wr_hbm.1, ...), custom_call_target="tpu_custom_call" | custom-call | tf_op jit(solution)/shard_map/up/pallas_call | solution.py:474
  43.1 0.0 copy-start
  43.1 12.1 %late.1 = bf16[192,128]{1,0:T(8,128)(2,1)S(1)} custom-call(s32[1,128]{1,0:T(1,128)} %get-tuple-element.109.act_ref, bf16[192,7168]{1,0:T(8,128)(2,1)} %get-tuple-element.110.late_hbm, bf16[32,7168,128]{2,1,0:T(8,128)(2,1)} %wg_hbm.3, bf16[32,7168,128]{2,1,0:T(8,128)(2,1)} %wu_hbm.3), custom_call_target="tpu_custom_call" | custom-call | tf_op jit(solution)/shard_map/late/pallas_call | solution.py:507
  55.2 0.0 copy-done
  55.2 55.9 %conditional.1 = (bf16[128,7168]{1,0:T(8,128)(2,1)S(1)}) conditional(s32[]{:T(128)} %bitcast.1, (bf16[320,128]{1,0:T(8,128)(2,1)S(1)}, bf16[192,128]{1,0:T(8,128)(2,1)S(1)}, bf16[128,7168]{1,0:T(8,128)(2,1)S(1)}, f32[128,2]{1,0:T(8,128)S(1)}, s32[4,8,128]{2,1,0:T(8,128)S(1)}, ...), branch_computations={%region_0.0_spmd, %region_1.0_spmd, %region_2.0_spmd, %region_3.0_... | conditional | bytes 8 | solution.py:568
  55.3 55.9 %down64_160.1 = bf16[128,7168]{1,0:T(8,128)(2,1)S(1)} custom-call(bf16[320,128]{1,0:T(8,128)(2,1)S(1)} %get-tuple-element.62.early_ref, bf16[192,128]{1,0:T(8,128)(2,1)S(1)} %get-tuple-element.70.late_ref, bf16[128,7168]{1,0:T(8,128)(2,1)S(1)} %get-tuple-element.72.x_ref, f32[128,2]{1,0:T(8,128)S(1)} %get-tuple-element.74.gate_ref, ...), custom_call_target="tpu_custom_call" | custom-call | tf_op jit(solution)/shard_map/cond/branch_0_fun/down64_160/pallas_call | solution.py:533
  111.2 1.2 %copy.24 = bf16[128,7168]{1,0:T(8,128)(2,1)} copy(bf16[128,7168]{1,0:T(8,128)(2,1)S(1)} %get-tuple-element.113) | data formatting | bytes 3670016
Async XLA Ops:
  43.1 12.1 %copy-start = (bf16[128,7168]{1,0:T(8,128)(2,1)S(1)}, bf16[128,7168]{1,0:T(8,128)(2,1)}, u32[]{:S(2)}) copy-start(bf16[128,7168]{1,0:T(8,128)(2,1)} %x_ref.1) | copy-start | bytes 5505028
